TPU v7x, 32 devices: a 4x4x1 block of a 4x4x8 slice. The times are simulated.
32 devices in a mesh: dp: 1 (over z), tp: 32 (over x, y, core).
Axes of the slice: x: 4, y: 4, z: 1, core: 2. Of those that a mesh axis runs over, the one named last changes fastest.
The devices are a block of a 4x4x8 slice.
Arguments:
- x: bfloat16 [5120, 7168], P(('dp', 'tp'))
- w_gate: bfloat16 [7168, 20480], P(None, 'tp')
- w_up: bfloat16 [7168, 20480], P(None, 'tp')
- w_down: bfloat16 [20480, 7168], P('tp')
Outputs:
- output: bfloat16 [5120, 7168], P(('dp', 'tp'))
All inputs are finite; a program needn't handle non-finite values.
Results may differ from a plain program's by a relative error of at most 0.016.
Values are sent between devices in bfloat16 or wider.
A program may use at most 768 MiB of HBM per device.

v0:
```python
import jax
import jax.numpy as jnp
from jax import lax
from jax.sharding import PartitionSpec as P


def solution(mesh):
    def step(x, w_gate, w_up, w_down):
        rows = lax.all_gather(x, "tp", axis=0, tiled=True)
        gate = jnp.dot(rows, w_gate, preferred_element_type=jnp.float32)
        up = jnp.dot(rows, w_up, preferred_element_type=jnp.float32)
        hidden = (jax.nn.silu(gate) * up).astype(jnp.bfloat16)
        term = jnp.dot(hidden, w_down, preferred_element_type=jnp.float32).astype(jnp.bfloat16)
        return lax.psum_scatter(term, "tp", scatter_dimension=0, tiled=True)

    return jax.shard_map(
        step,
        mesh=mesh,
        in_specs=(P(("dp", "tp"), None), P(None, "tp"), P(None, "tp"), P("tp", None)),
        out_specs=P(("dp", "tp"), None),
        check_vma=False,
    )
```

profile of v0, /device:TPU:97, one launch (start us, length us, event | category | flops | bytes accessed | tf_op | source)
XLA Modules:
  0.0 731.9 jit_solution(5921884446904067049)
XLA Ops:
  6.5 0.0 all-gather.2.cloned.1.call-start
  6.6 0.7 all-gather.2.cloned.1.call-update
  7.3 0.1 reduce-scatter.4.cloned.1.call-start
  7.4 218.6 %all-gather.2.cloned.1.call-done = bf16[5120,7168]{1,0:T(8,128)(2,1)} async-done(((bf16[160,7168]{1,0:T(8,128)(2,1)}), bf16[5120,7168]{1,0:T(8,128)(2,1)}) %all-gather.2.cloned.1.call-update) | async-done | bytes 73400336 | tf_op jit(solution)/shard_map/all_gather | solution.py:9
  226.0 65.1 %fusion = f32[5120,640]{1,0:T(8,128)S(1)} fusion(bf16[5120,7168]{1,0:T(8,128)(2,1)} %all-gather.2.cloned.1.call-done, bf16[7168,640]{1,0:T(8,128)(2,1)} %param.5), kind=kOutput, calls=%fused_computation.2 | convolution fusion | flops 46976204800 | bytes 95682560 | tf_op jit(solution)/shard_map/dot_general | solution.py:10
  291.1 65.7 %multiply_convert_fusion = bf16[5120,640]{1,0:T(8,128)(2,1)} fusion(f32[5120,640]{1,0:T(8,128)S(1)} %fusion, bf16[5120,7168]{1,0:T(8,128)(2,1)} %all-gather.2.cloned.1.call-done, bf16[7168,640]{1,0:T(8,128)(2,1)} %param.6), kind=kOutput, calls=%fused_computation.1 | convolution fusion | flops 46995865600 | bytes 102236160 | tf_op jit(solution)/shard_map/dot_general | solution.py:11
  356.8 65.8 %convolution_convert_fusion = bf16[5120,7168]{1,0:T(8,128)(2,1)} fusion(bf16[5120,640]{1,0:T(8,128)(2,1)} %multiply_convert_fusion, bf16[640,7168]{1,0:T(8,128)(2,1)} %param.7), kind=kOutput, calls=%fused_computation | convolution fusion | flops 47012904960 | bytes 89128960 | tf_op jit(solution)/shard_map/dot_general | solution.py:13
  422.6 0.1 reduce-scatter.4.cloned.1.call-update
  422.7 302.3 %reduce-scatter.4.cloned.1.call-done = bf16[160,7168]{1,0:T(8,128)(2,1)} async-done(((bf16[5120,7168]{1,0:T(8,128)(2,1)}), bf16[160,7168]{1,0:T(8,128)(2,1)}) %reduce-scatter.4.cloned.1.call-update) | async-done | bytes 2293776
Async XLA Ops:
  6.5 219.4 %all-gather.2.cloned.1.call-start = ((), (), s32[]{:S(2)}) async-start(), calls=%async_computation.1 | async-start | bytes 75694080 | tf_op jit(solution)/shard_map/all_gather | solution.py:9
  7.3 717.7 %reduce-scatter.4.cloned.1.call-start = ((), (), s32[]{:S(2)}) async-start(), calls=%async_computation.2 | async-start | bytes 75694080
Sparse Core Ops, SparseCore 0:
  9.4 216.4 all-gather.1
  422.8 302.1 reduce-scatter.3
where the time goes:
time: 732 us
  waiting for transfers between devices  522 us (71%)
  matrix products  197 us (27%)
  between operations  13.4 us (2%)
    unnamed x3, waiting for transfers between devices  303 us
    all_gather x1, waiting for transfers between devices, step(): rows = lax.all_gather(x, 'tp', axis=0, tiled=True)  219 us
    dot_general x1, matrix products, step(): jnp.dot(hidden, w_down, preferred_element_type=jnp.float32)  65.8 us
    dot_general x1, matrix products, step(): up = jnp.dot(rows, w_up, preferred_element_type=jnp.float32)  65.7 us
    dot_general x1, matrix products, step(): gate = jnp.dot(rows, w_gate, preferred_element_type=jnp.float32)  65.1 us
  transfers between devices with their start and end apart: 2, of which 2 were waited for; matrix products, arithmetic and copies ran while one was open for 0% of the time, Pallas kernels for 0%

commit v1 on v0

v1 whole, which is shorter than its diff:
```python
import functools
import math

import jax
import jax.numpy as jnp
from jax import lax
from jax.experimental import pallas as pl
from jax.experimental.pallas import tpu as pltpu
from jax.sharding import PartitionSpec as P

RING = 4
LANES = 128
TILE = 512


def _offset(k):
    return k + lax.div(k, 2) - 2 * lax.div(k, 3)


def _place(j):
    p = lax.div(j + 4, 8)
    w0, w1, w2 = lax.div((1 - p) * (2 - p), 2), p * (2 - p), lax.div(p * (p - 1), 2)
    k = w0 * j + w1 * (lax.div(j + 4, 2) - 4) + w2 * (j - 12)
    return _offset(k), w1 * (3 - 2 * lax.rem(j, 2)) + 2 * w2


def _device(a, b, c):
    x = a * (1 - c) + b * c
    y = b * (1 - c) + a * c
    return (x * RING + y) * 2 + c


def _kernel(
    x, w_gate, w_up, w_down,
    y, xg, pb, rb, rh,
    wgu, wd, h, xb, stq, sto, ib,
    w_sem, x_send, x_recv, d_send, d_recv, p_send, p_recv, rb_send, rb_recv, rh_send, rh_recv, ld_sem,
):
    rows, cols = x.shape
    half = rows // 2
    chunks = w_gate.shape[1] // LANES
    blocks = RING * RING
    lo, hi = pl.ds(0, half), pl.ds(half, half)
    halves = (lo, hi)

    me = lax.axis_index("tp")
    c = lax.rem(me, 2)
    chip = lax.div(me, 2)
    px, py = lax.div(chip, RING), lax.rem(chip, RING)
    a = px * (1 - c) + py * c
    b = py * (1 - c) + px * c

    def turn(v, d):
        return lax.rem(v + d, RING)

    a_right, a_left = _device(turn(a, 1), b, c), _device(turn(a, RING - 1), b, c)
    b_right, b_left = _device(a, turn(b, 1), c), _device(a, turn(b, RING - 1), c)
    partner = me + 1 - 2 * c

    def own(j):
        da, db = _place(j)
        return _device(turn(a, da), turn(b, db), c)

    def theirs(j):
        da, db = _place(j)
        return _device(turn(b, da), turn(a, db), 1 - c)

    def remote(src, dst, send, recv, device):
        return pltpu.make_async_remote_copy(
            src_ref=src, dst_ref=dst, send_sem=send, recv_sem=recv,
            device_id={"tp": device}, device_id_type=pl.DeviceIdType.MESH,
        )

    def weight_copies():
        for n in range(chunks):
            part = pl.ds(n * LANES, LANES)
            yield pltpu.make_async_copy(w_gate.at[:, part], wgu.at[n, :, pl.ds(0, LANES)], w_sem.at[2 * n])
            yield pltpu.make_async_copy(w_up.at[:, part], wgu.at[n, :, pl.ds(LANES, LANES)], w_sem.at[2 * n + 1])
        yield pltpu.make_async_copy(w_down, wd, w_sem.at[2 * chunks])

    barrier = pltpu.get_barrier_semaphore()
    peers = (partner, a_right, a_left, b_right, b_left)
    for peer in peers:
        pl.semaphore_signal(barrier, inc=1, device_id={"tp": peer}, device_id_type=pl.DeviceIdType.MESH)
    pl.semaphore_wait(barrier, len(peers))

    def ring(src, block, i, j, device):
        return remote(src, xg.at[block, halves[i]], x_send.at[j, i], x_recv.at[j, i], device)

    def arrived(j, i):
        slot = xg.at[own(j), halves[i]]
        remote(slot, slot, x_send.at[j, i], x_recv.at[j, i], me).wait_recv()

    def both_ways(src, block, k):
        for i in (0, 1):
            ring(src.at[halves[i]], block, i, 4 + 2 * k, b_right).start()
            ring(src.at[halves[1 - i]], block, 1 - i, 5 + 2 * k, b_left).start()

    def hand_over(src, block, j):
        return remote(src, xg.at[block], d_send.at[j], d_recv.at[j], partner)

    for i in (0, 1):
        ring(x.at[halves[i]], me, i, 2, a_right).start()
        ring(x.at[halves[1 - i]], me, 1 - i, 1, a_left).start()
    hand_over(x, me, 0).start()
    for copy in weight_copies():
        copy.start()
    arrived(1, 1)
    ring(xg.at[own(1), hi], own(1), 1, 3, a_left).start()
    arrived(2, 0)
    ring(xg.at[own(2), lo], own(2), 0, 3, a_right).start()
    both_ways(x, me, 0)
    for copy in weight_copies():
        copy.wait()

    unroll = max(u for u in range(1, 8) if (cols // TILE) % u == 0)

    def down(block, first, count, adds, out):
        def body(i, _):
            for u in range(unroll):
                part = pl.ds(pl.multiple_of((i * unroll + u) * TILE, TILE), TILE)
                acc = jnp.dot(
                    h[block, pl.ds(first, count), :], wd[:, part], preferred_element_type=jnp.float32
                )
                edges = sorted({first, first + count} | {e for _, _, s, t in adds for e in (s, t)})
                for s, t in zip(edges, edges[1:]):
                    piece = acc[s - first : t - first]
                    for ref, row, s1, t1 in adds:
                        if s1 <= s and t <= t1:
                            piece += ref[pl.ds(row + s - s1, t - s), part].astype(jnp.float32)
                    out[pl.ds(s, t - s), part] = piece.astype(out.dtype)
            return 0

        lax.fori_loop(0, cols // (TILE * unroll), body, 0)

    def load(src, dst, sem):
        return pltpu.make_async_copy(src, dst, ld_sem.at[sem])

    def term_arrived(j):
        remote(pb.at[j], pb.at[j], p_send.at[0], p_recv.at[j], me).wait_recv()

    def sum_hop(src, whole, slot, device):
        dst, send, recv = (rb, rb_send, rb_recv) if whole else (rh, rh_send, rh_recv)
        return remote(src, dst.at[slot], send.at[slot], recv.at[slot], device)

    def last_hop(src, i, slot, device):
        s = 8 + 2 * (slot - 8) + i
        return remote(src, rb.at[slot, halves[i]], rb_send.at[s], rb_recv.at[s], device)

    def sum_arrived(whole, slot):
        dst = rb if whole else rh
        sum_hop(dst.at[slot], whole, slot, me).wait_recv()

    def step(s, _):
        mine, other = xb.at[pl.ds(0, rows)], xb.at[pl.ds(rows, rows)]
        stage = lax.rem(s, 2)

        @pl.when(s == 0)
        def _():
            load(x, mine, 0).start()

        @pl.when((s >= 1) & (s <= 3))
        def _():
            @pl.when(s == 1)
            def _():
                arrived(1, 0)

            @pl.when(s == 2)
            def _():
                arrived(2, 1)

            @pl.when(s == 3)
            def _():
                arrived(3, 0)
                arrived(3, 1)

            both_ways(xg.at[own(s)], own(s), s)

        @pl.when((s >= 4) & (s <= 11))
        def _():
            k = lax.div(s - 4, 2)

            @pl.when(lax.rem(s, 2) == 0)
            def _():
                arrived(s, 0)
                ring(xg.at[own(s), lo], own(s), 0, 12 + k, b_right).start()
                arrived(s, 1)

            @pl.when(lax.rem(s, 2) == 1)
            def _():
                arrived(s, 1)
                ring(xg.at[own(s), hi], own(s), 1, 12 + k, b_left).start()
                arrived(s, 0)

        @pl.when((s >= 12) & (s <= 15))
        def _():
            arrived(s, 0)
            arrived(s, 1)

        @pl.when((s >= 1) & (s <= 15))
        def _():
            load(xg.at[own(s)], mine, 0).start()
            hand_over(xg.at[own(s)], own(s), s).start()

        @pl.when((s >= 1) & (s <= 16))
        def _():
            block = theirs(s - 1)
            remote(xg.at[block], xg.at[block], d_send.at[s - 1], d_recv.at[s - 1], me).wait_recv()
            load(xg.at[block], other, 1).start()

        @pl.when(s >= 2)
        def _():
            j = s - 2
            copy = remote(stq.at[stage], pb.at[j], p_send.at[stage], p_recv.at[j], partner)

            @pl.when(s >= 4)
            def _():
                copy.wait_send()

            down(blocks + j, 0, rows, (), stq.at[stage])
            copy.start()

        @pl.when(s <= 15)
        def _():
            load(x, mine, 0).wait()

        @pl.when((s >= 1) & (s <= 16))
        def _():
            load(x, other, 1).wait()

        @pl.when(s <= 16)
        def _():
            for n in range(chunks):
                acc = jnp.dot(xb[...], wgu[n], preferred_element_type=jnp.float32)
                part = pl.ds(n * LANES, LANES)
                hid = (jax.nn.silu(acc[:, :LANES]) * acc[:, LANES:]).astype(h.dtype)

                h[s + (blocks + 1) * lax.div(s, blocks), :, part] = hid[:rows]
                h[lax.rem(s + blocks, blocks + 1) + blocks, :, part] = hid[rows:]

        @pl.when(s >= 14)
        def _():
            j, k = s - 2, s - 14
            term_arrived(j)
            load(pb.at[j], ib.at[0], 0).start()
            load(pb.at[j], ib.at[0], 0).wait()
            down(j, 0, rows, ((ib.at[0], 0, 0, rows),), sto.at[k])
            sum_hop(sto.at[k, lo], False, k, b_right).start()
            sum_hop(sto.at[k, hi], False, 4 + k, b_left).start()

        return 0

    lax.fori_loop(0, blocks + 2, step, 0)

    def near(i, _):
        k = lax.rem(i + 1, 4)
        right, left = 2 * lax.rem(i, 2), 2 * lax.rem(i, 2) + 1
        for d, slot in ((1, right), (0, left)):
            j = 4 + 2 * k + d
            came = k if d else 4 + k

            @pl.when(i < 2)
            def _():
                sum_hop(sto.at[slot, lo], False, slot, me).wait_send()
                sum_hop(sto.at[slot, hi], False, 4 + slot, me).wait_send()

            @pl.when(i >= 2)
            def _():
                sum_hop(sto.at[slot], True, (i - 1) + 4 * (1 - d), me).wait_send()

            term_arrived(j)
            first = load(pb.at[j], ib.at[0], 0)
            first.start()
            sum_arrived(False, came)
            second = load(rh.at[came], ib.at[1, lo], 1)
            second.start()
            first.wait()
            second.wait()
            part = (0, half) if d else (half, rows)
            down(j, 0, rows, ((ib.at[0], 0, 0, rows), (ib.at[1], 0, *part)), sto.at[slot])
            sum_hop(sto.at[slot], True, k if d else 4 + k, b_right if d else b_left).start()
        return 0

    lax.fori_loop(0, 4, near, 0)

    def gather_terms(k):
        term_arrived(k)
        sum_arrived(True, k)
        sum_arrived(True, 4 + k)
        copies = [load(pb.at[k], ib.at[0], 0), load(rb.at[k], ib.at[1], 1), load(rb.at[4 + k], ib.at[2], 2)]
        for copy in copies:
            copy.start()
        for copy in copies:
            copy.wait()

    three = tuple((ib.at[i], 0, 0, rows) for i in range(3))

    def rows_of(adds, s, t):
        return tuple((ref, s, s, t) for ref, _, _, _ in adds)

    sum_hop(sto.at[0], True, 3, me).wait_send()
    gather_terms(3)
    down(3, 0, rows, three, sto.at[0])
    sum_hop(sto.at[0, lo], False, 8, a_right).start()
    sum_hop(sto.at[0, hi], False, 9, a_left).start()

    sum_hop(sto.at[1], True, 7, me).wait_send()
    gather_terms(1)
    down(1, half, half, rows_of(three, half, rows), sto.at[1])
    last_hop(sto.at[1, hi], 1, 8, a_right).start()
    sum_arrived(False, 8)
    extra = load(rh.at[8], xb.at[lo], 3)
    extra.start()
    extra.wait()
    down(1, 0, half, rows_of(three, 0, half) + ((xb, 0, 0, half),), sto.at[1])
    last_hop(sto.at[1, lo], 0, 8, a_right).start()

    sum_hop(sto.at[2], True, 0, me).wait_send()
    gather_terms(2)
    down(2, 0, half, rows_of(three, 0, half), sto.at[2])
    last_hop(sto.at[2, lo], 0, 9, a_left).start()
    sum_arrived(False, 9)
    extra = load(rh.at[9], xb.at[lo], 3)
    extra.start()
    extra.wait()
    down(2, half, half, rows_of(three, half, rows) + ((xb, 0, half, rows),), sto.at[2])
    last_hop(sto.at[2, hi], 1, 9, a_left).start()

    sum_hop(sto.at[3], True, 4, me).wait_send()
    gather_terms(0)
    for slot in (8, 9):
        for i in (0, 1):
            last_hop(rb.at[slot, halves[i]], i, slot, me).wait_recv()
    extras = [load(rb.at[8 + i], xb.at[pl.ds(i * rows, rows)], 3 + i) for i in range(2)]
    for copy in extras:
        copy.start()
    for copy in extras:
        copy.wait()
    down(0, 0, rows, three + ((xb, 0, 0, rows), (xb, rows, 0, rows)), sto.at[3])
    out = load(sto.at[3], y, 0)
    out.start()

    for j in range(1, blocks):
        for i in (0, 1):
            remote(xg.at[0, lo], xg.at[0, lo], x_send.at[j, i], x_recv.at[j, i], me).wait_send()
    for j in range(blocks):
        remote(xg.at[0], xg.at[0], d_send.at[j], d_recv.at[j], me).wait_send()
    for stage in range(2):
        remote(stq.at[stage], pb.at[0], p_send.at[stage], p_recv.at[0], me).wait_send()
    for slot, part in ((8, lo), (9, hi)):
        sum_hop(sto.at[0, part], False, slot, me).wait_send()
    for slot in (8, 9):
        for i in (0, 1):
            last_hop(sto.at[slot - 7, halves[i]], i, slot, me).wait_send()
    out.wait()


def solution(mesh):
    n = mesh.shape["tp"]
    if n != 2 * RING * RING:
        raise ValueError("ring size")

    def block(x, w_gate, w_up, w_down):
        rows, cols = x.shape
        hidden = w_gate.shape[1]
        dma = pltpu.SemaphoreType.DMA
        chunks = hidden // LANES
        flops = 6 * n * rows * cols * hidden
        any_spec = pl.BlockSpec(memory_space=pl.ANY)
        out = pl.pallas_call(
            _kernel,
            out_shape=(
                jax.ShapeDtypeStruct((rows, cols), x.dtype),
                jax.ShapeDtypeStruct((n, rows, cols), x.dtype),
                jax.ShapeDtypeStruct((n // 2, rows, cols), x.dtype),
                jax.ShapeDtypeStruct((10, rows, cols), x.dtype),
                jax.ShapeDtypeStruct((10, rows // 2, cols), x.dtype),
            ),
            in_specs=[any_spec] * 4,
            out_specs=[any_spec] * 5,
            scratch_shapes=[
                pltpu.VMEM((chunks, cols, 2 * LANES), x.dtype),
                pltpu.VMEM((hidden, cols), x.dtype),
                pltpu.VMEM((n + 2, rows, hidden), x.dtype),
                pltpu.VMEM((2 * rows, cols), x.dtype),
                pltpu.VMEM((2, rows, cols), x.dtype),
                pltpu.VMEM((4, rows, cols), x.dtype),
                pltpu.VMEM((3, rows, cols), x.dtype),
                dma((2 * chunks + 1,)),
                dma((n // 2, 2)),
                dma((n // 2, 2)),
                dma((n // 2,)),
                dma((n // 2,)),
                dma((2,)),
                dma((n // 2,)),
                dma((12,)),
                dma((12,)),
                dma((10,)),
                dma((10,)),
                dma((5,)),
            ],
            compiler_params=pltpu.CompilerParams(
                collective_id=0, has_side_effects=True, vmem_limit_bytes=67_000_000
            ),
            cost_estimate=pl.CostEstimate(flops=flops, bytes_accessed=8 * n * rows * cols, transcendentals=0),
        )(x, w_gate, w_up, w_down)
        return out[0]

    return jax.shard_map(
        block,
        mesh=mesh,
        in_specs=(P(("dp", "tp"), None), P(None, "tp"), P(None, "tp"), P("tp", None)),
        out_specs=P(("dp", "tp"), None),
        check_vma=False,
    )
```

time: 732 us -> 401 us (0.55)
  waiting for transfers between devices: 522 us -> 0 us
  Pallas kernels: 0 us -> 396 us
  matrix products: 197 us -> 0 us
  between operations: 13.4 us -> 0.01 us
    pallas_call x0 -> x1, Pallas kernels: none -> 396 us  [block(): pl.pallas_call(_kernel, out_shape=(jax.ShapeDtypeStruct((rows, cols), x.d...]
    unnamed x3 -> x0, waiting for transfers between devices: 303 us -> none
    all_gather x1 -> x0, waiting for transfers between devices: 219 us -> none  [step(): rows = lax.all_gather(x, 'tp', axis=0, tiled=True)]
    dot_general x3 -> x0, matrix products: 197 us -> none  [the longest x1 65.8 us: step(): jnp.dot(hidden, w_down, preferred_element_type=jnp.float32)]
  transfers between devices with their start and end apart: 2 -> 0, of which waited for: 2 -> 0; matrix products, arithmetic and copies ran while one was open for 0% -> 0% of each run, Pallas kernels for 0% -> 0%
where the time goes in v1:
time: 401 us; the launch traced here: 400 us
  Pallas kernels  396 us (99%)
    pallas_call x1, Pallas kernels, block(): pl.pallas_call(_kernel, out_shape=(jax.ShapeDtypeStruct((rows, cols), x.d...  396 us

profile of v1, /device:TPU:97, one launch (start us, length us, event | category | flops | bytes accessed | tf_op | source)
XLA Modules:
  0.0 399.5 jit_solution(846521207601909053)
XLA Ops:
  0.0 396.3 %shard_map.46 = (bf16[160,7168]{1,0:T(8,128)(2,1)}, bf16[32,160,7168]{2,1,0:T(8,128)(2,1)}, bf16[16,160,7168]{2,1,0:T(8,128)(2,1)}, bf16[10,160,7168]{2,1,0:T(8,128)(2,1)}, bf16[10,80,7168]{2,1,0:T(8,128)(2,1)}) custom-call(bf16[160,7168]{1,0:T(8,128)(2,1)} %x.1, bf16[7168,640]{1,0:T(8,128)(2,1)} %w_gate.1, bf16[7168,640]{1,0:T(8,128)(2,1)} %w_up.1, ...), custom_call_target="tpu_custom_call" | custom-call | flops 140928614400 | bytes 293601280 | tf_op jit(solution)/shard_map/pallas_call | solution.py:370
  396.3 3.2 copy.6
